TPU v7x, 8 devices: a whole 2x2x1 slice. The times are simulated.
8 devices in a mesh: tp: 4 (over z, y, x), dp: 2 (over core).
Axes of the slice: x: 2, y: 2, z: 1, core: 2. Of those that a mesh axis runs over, the one named last changes fastest.
Arguments:
- hidden_in: bfloat16 [4096, 2560], P('dp')
- targets: bfloat16 [4096, 2560], P('dp')
- w_up: bfloat16 [4, 2560, 10240], P(None, None, 'tp')
- w_down: bfloat16 [4, 10240, 2560], P(None, 'tp')
Outputs:
- output 1: float32 [4, 2560, 10240], P(None, None, 'tp')
- output 2: float32 [4, 10240, 2560], P(None, 'tp')
All inputs are finite; a program needn't handle non-finite values.
Results may differ from a plain program's by a relative error of at most 0.0121431.
Values are sent between devices in bfloat16 or wider.
A program may use at most 1.25 GiB of HBM per device.

v0:
```python
import functools
import jax
import jax.numpy as jnp
from jax import lax
from jax.sharding import PartitionSpec as P

ROW_CONTRACT = (((0,), (0,)), ((), ()))
COL_CONTRACT = (((1,), (1,)), ((), ()))


def gelu_tanh(value):
    return jax.nn.gelu(value, approximate=True)


def local_step(hidden, targets, w_up, w_down, total_tokens):
    layers = w_up.shape[0]
    h_cur = hidden
    saved = []
    for layer in range(layers):
        pre_act = jnp.dot(h_cur, w_up[layer], preferred_element_type=jnp.float32).astype(jnp.bfloat16)
        act_val = gelu_tanh(pre_act.astype(jnp.float32)).astype(jnp.bfloat16)
        part_out = jnp.dot(act_val, w_down[layer], preferred_element_type=jnp.float32)
        branch = lax.psum(part_out, "tp").astype(jnp.bfloat16)
        saved.append((h_cur, pre_act, act_val))
        h_cur = h_cur + branch
    err_f32 = (h_cur.astype(jnp.float32) - targets.astype(jnp.float32)) / total_tokens
    g_cur = err_f32.astype(jnp.bfloat16)
    grads_up = [None] * layers
    grads_down = [None] * layers
    for layer in reversed(range(layers)):
        h_in, pre_act, act_val = saved[layer]
        g_down = lax.dot_general(act_val, g_cur, ROW_CONTRACT, preferred_element_type=jnp.float32)
        grads_down[layer] = lax.psum(g_down, "dp")
        d_act = lax.dot_general(g_cur, w_down[layer], COL_CONTRACT, preferred_element_type=jnp.float32)
        _, gelu_vjp = jax.vjp(gelu_tanh, pre_act.astype(jnp.float32))
        d_pre = gelu_vjp(d_act)[0].astype(jnp.bfloat16)
        g_up = lax.dot_general(h_in, d_pre, ROW_CONTRACT, preferred_element_type=jnp.float32)
        grads_up[layer] = lax.psum(g_up, "dp")
        if layer > 0:
            back_part = lax.dot_general(d_pre, w_up[layer], COL_CONTRACT, preferred_element_type=jnp.float32)
            g_cur = (g_cur.astype(jnp.float32) + lax.psum(back_part, "tp")).astype(jnp.bfloat16)
    return jnp.stack(grads_up), jnp.stack(grads_down)


def solution(mesh):
    def grad_step(hidden_in, targets, w_up, w_down):
        step_fn = functools.partial(local_step, total_tokens=hidden_in.shape[0])
        mapped = jax.shard_map(step_fn, mesh=mesh, in_specs=(P("dp", None), P("dp", None), P(None, None, "tp"), P(None, "tp", None)), out_specs=(P(None, None, "tp"), P(None, "tp", None)), check_vma=False)
        return mapped(hidden_in, targets, w_up, w_down)

    return grad_step
```

profile of v0, /device:TPU:0, one launch (start us, length us, event | category | flops | bytes accessed | tf_op | source)
XLA Modules:
  0.0 5150.6 jit_solution(6563325455129144950)
XLA Ops:
  7.2 32.9 fusion.85
  44.0 41.8 fusion.66
  85.8 696.4 %all-reduce.21 = bf16[2048,2560]{1,0:T(8,128)(2,1)} all-reduce(f32[2048,2560]{1,0:T(8,128)} %fusion.66), channel_id=1, replica_groups=mesh['tp'=4,'dp'=2] {'tp'}, use_global_device_ids=true, to_apply=%region_0.0 | all-reduce | flops 5242880 | bytes 31457280 | tf_op jit(solution)/shard_map/psum | solution.py:23
  828.8 41.8 fusion.58
  870.6 691.1 %all-reduce.22 = bf16[2048,2560]{1,0:T(8,128)(2,1)} all-reduce(f32[2048,2560]{1,0:T(8,128)} %fusion.58), channel_id=1, replica_groups=mesh['tp'=4,'dp'=2] {'tp'}, use_global_device_ids=true, to_apply=%region_1.0 | all-reduce | flops 5242880 | bytes 31457280 | tf_op jit(solution)/shard_map/psum | solution.py:23
  1608.4 42.0 fusion.50
  1650.4 689.5 %all-reduce.23 = bf16[2048,2560]{1,0:T(8,128)(2,1)} all-reduce(f32[2048,2560]{1,0:T(8,128)} %fusion.50), channel_id=1, replica_groups=mesh['tp'=4,'dp'=2] {'tp'}, use_global_device_ids=true, to_apply=%region_2.0 | all-reduce | flops 5242880 | bytes 31457280 | tf_op jit(solution)/shard_map/psum | solution.py:23
  2386.6 42.0 fusion.42
  2428.6 689.6 %all-reduce.24 = bf16[2048,2560]{1,0:T(8,128)(2,1)} all-reduce(f32[2048,2560]{1,0:T(8,128)} %fusion.42), channel_id=1, replica_groups=mesh['tp'=4,'dp'=2] {'tp'}, use_global_device_ids=true, to_apply=%region_3.0 | all-reduce | flops 5242880 | bytes 31457280 | tf_op jit(solution)/shard_map/psum | solution.py:23
  3131.6 46.0 fusion.6
  3177.6 35.3 fusion.44
  3212.9 364.8 %all-reduce.12.cloned.1.call-done = f32[2048,2560]{1,0:T(8,128)} async-done(((f32[2048,2560]{1,0:T(8,128)}), f32[2048,2560]{1,0:T(8,128)}) %all-reduce.12.cloned.1.call-update) | async-done | bytes 20971536 | tf_op jit(solution)/shard_map/psum | solution.py:41
  3589.0 46.9 fusion.9
  3639.8 32.2 fusion.52
  3672.1 363.9 %all-reduce.14.cloned.1.call-done = f32[2048,2560]{1,0:T(8,128)} async-done(((f32[2048,2560]{1,0:T(8,128)}), f32[2048,2560]{1,0:T(8,128)}) %all-reduce.14.cloned.1.call-update) | async-done | bytes 20971536 | tf_op jit(solution)/shard_map/psum | solution.py:41
  4047.7 46.9 fusion.12
  4098.5 32.2 fusion.60
  4130.8 35.9 convolution_bitcast_fusion.4
  4166.7 36.0 convolution_bitcast_fusion.5
  4202.7 32.9 convolution_bitcast_fusion.6
  4235.6 259.1 %all-reduce.16.cloned.1.call-done = f32[2048,2560]{1,0:T(8,128)} async-done(((f32[2048,2560]{1,0:T(8,128)}), f32[2048,2560]{1,0:T(8,128)}) %all-reduce.16.cloned.1.call-update) | async-done | bytes 20971536 | tf_op jit(solution)/shard_map/psum | solution.py:41
  4494.7 36.7 fusion.64
  4531.4 47.4 convolution_bitcast_fusion.7
  4578.9 38.6 convolution_bitcast_fusion
  4617.6 36.5 convolution_bitcast_fusion.1
  4654.1 36.5 convolution_bitcast_fusion.2
  4690.6 47.2 convolution_bitcast_fusion.3
  4737.9 87.5 %all-reduce.18.cloned.1.call-done = (f32[1,2560,2560]{1,2,0:T(8,128)}, f32[1,2560,2560]{1,2,0:T(8,128)}, f32[1,2560,2560]{1,2,0:T(8,128)}, f32[1,2560,2560]{1,2,0:T(8,128)}) async-done(((f32[1,2560,2560]{1,2,0:T(8,128)}, f32[1,2560,2560]{1,2,0:T(8,128)}, f32[1,2560,2560]{1,2,0:T(8,128)}, f32[1,2560,2560]{1,2,0:T(8,128)}), (f32[1,2560,2560]{1,2,0:T(8,128)}, f32[1,2560,2560]{1,2,0:T(8,128)}, ...) | async-done | bytes 104857616 | tf_op jit(solution)/shard_map/psum | solution.py:38
  4825.4 68.5 %pad_maximum_fusion = f32[4,2560,2560]{1,2,0:T(8,128)} fusion(f32[1,2560,2560]{1,2,0:T(8,128)} %get-tuple-element.4, f32[1,2560,2560]{1,2,0:T(8,128)} %get-tuple-element.5, f32[1,2560,2560]{1,2,0:T(8,128)} %get-tuple-element.6, f32[1,2560,2560]{1,2,0:T(8,128)} %get-tuple-element.7), kind=kLoop, calls=%fused_computation | loop fusion | flops 78643200 | bytes 209715200 | tf_op jit(solution)/shard_map/stack | solution.py:42
  4893.9 100.8 %copy.9 = f32[4,2560,2560]{2,1,0:T(8,128)} copy(f32[4,2560,2560]{1,2,0:T(8,128)} %pad_maximum_fusion) | data formatting | bytes 209715200
  4994.6 80.4 %all-reduce.20.cloned.1.call-done = (f32[1,2560,2560]{2,1,0:T(8,128)}, f32[1,2560,2560]{2,1,0:T(8,128)}, f32[1,2560,2560]{2,1,0:T(8,128)}, f32[1,2560,2560]{2,1,0:T(8,128)}) async-done(((f32[1,2560,2560]{2,1,0:T(8,128)}, f32[1,2560,2560]{2,1,0:T(8,128)}, f32[1,2560,2560]{2,1,0:T(8,128)}, f32[1,2560,2560]{2,1,0:T(8,128)}), (f32[1,2560,2560]{2,1,0:T(8,128)}, f32[1,2560,2560]{2,1,0:T(8,128)}, ...) | async-done | bytes 104857616 | tf_op jit(solution)/shard_map/psum | solution.py:33
  5075.1 68.5 %pad_maximum_fusion.1 = f32[4,2560,2560]{2,1,0:T(8,128)} fusion(f32[1,2560,2560]{2,1,0:T(8,128)} %get-tuple-element.8, f32[1,2560,2560]{2,1,0:T(8,128)} %get-tuple-element.9, f32[1,2560,2560]{2,1,0:T(8,128)} %get-tuple-element.10, f32[1,2560,2560]{2,1,0:T(8,128)} %get-tuple-element.11), kind=kLoop, calls=%fused_computation.1 | loop fusion | flops 78643200 | bytes 209715200 | tf_op jit(solution)/shard_map/stack | solution.py:42
  (61 shorter events, 188.0 us)
Async XLA Ops:
  7.2 3570.5 %all-reduce.12.cloned.1.call-start = ((), (), s32[]{:S(2)}) async-start(), calls=%async_computation | async-start | bytes 41943040 | tf_op jit(solution)/shard_map/psum | solution.py:41
  40.2 3.9 copy-start.7
  791.1 3.9 copy-start.4
  824.9 3.9 copy-start.8
  1570.6 4.0 copy-start.5
  1604.5 3.9 copy-start.9
  2348.7 4.1 copy-start.3
  2382.7 3.9 copy-start.10
  3118.3 13.3 copy-start.11
  3131.6 46.0 copy-start
  3212.9 823.1 %all-reduce.14.cloned.1.call-start = ((), (), s32[]{:S(2)}) async-start(), calls=%async_computation.1 | async-start | bytes 41943040 | tf_op jit(solution)/shard_map/psum | solution.py:41
  3589.0 46.9 copy-start.1
  3635.9 3.9 copy-start.12
  3672.0 822.7 %all-reduce.16.cloned.1.call-start = ((), (), s32[]{:S(2)}) async-start(), calls=%async_computation.2 | async-start | bytes 41943040 | tf_op jit(solution)/shard_map/psum | solution.py:41
  4047.7 46.9 copy-start.6
  4094.6 3.9 copy-start.13
  4130.8 694.6 %all-reduce.18.cloned.1.call-start = ((), (), s32[]{:S(2)}) async-start(), calls=%async_computation.3 | async-start | bytes 209715200 | tf_op jit(solution)/shard_map/psum | solution.py:38
  4130.8 71.9 %slice-start = ((s8[10485760]{0:T(1024)(128)(4,1)}), s8[4194304]{0:T(1024)(128)(4,1)S(1)}, s32[]{:S(2)}) async-start(s8[10485760]{0:T(1024)(128)(4,1)} %bitcast.90), calls=%async_computation.5 | async-start | bytes 8388608
  4130.8 71.9 %slice-start.1 = ((s8[10485760]{0:T(1024)(128)(4,1)}), s8[4194304]{0:T(1024)(128)(4,1)S(1)}, s32[]{:S(2)}) async-start(s8[10485760]{0:T(1024)(128)(4,1)} %bitcast.90), calls=%async_computation.6 | async-start | bytes 8388608
  4166.7 36.0 slice-start.2
  4578.8 496.2 %all-reduce.20.cloned.1.call-start = ((), (), s32[]{:S(2)}) async-start(), calls=%async_computation.4 | async-start | bytes 209715200 | tf_op jit(solution)/shard_map/psum | solution.py:33
  4578.9 38.7 copy-start.2
  4578.9 75.1 %slice-start.3 = ((s8[10485760]{0:T(1024)(128)(4,1)}), s8[4194304]{0:T(1024)(128)(4,1)S(1)}, s32[]{:S(2)}) async-start(s8[10485760]{0:T(1024)(128)(4,1)} %bitcast.92), calls=%async_computation.8 | async-start | bytes 8388608
  4578.9 75.1 %slice-start.4 = ((s8[10485760]{0:T(1024)(128)(4,1)}), s8[4194304]{0:T(1024)(128)(4,1)S(1)}, s32[]{:S(2)}) async-start(s8[10485760]{0:T(1024)(128)(4,1)} %bitcast.92), calls=%async_computation.9 | async-start | bytes 8388608
  4617.6 36.5 slice-start.5
Sparse Core Ops, SparseCore 0:
  3213.0 364.6 all-reduce.11
  3672.2 363.7 all-reduce.13
  4130.9 363.7 all-reduce.15
  4579.0 246.3 all-reduce.17
  4828.0 246.9 all-reduce.19
where the time goes:
time: 5160 us; the launch traced here: 5150 us
  blocking collectives  2770 us (54%)
  waiting for transfers between devices  1160 us (22%)
  matrix products  877 us (17%)
  other arithmetic  199 us (4%)
  local copies, waits for them, and re-layouts  137 us (3%)
    psum x4, blocking collectives, local_step(): branch = lax.psum(part_out, 'tp').astype(jnp.bfloat16)  2770 us
    psum x3, waiting for transfers between devices, local_step(): lax.psum(back_part, 'tp')  988 us
    dot_general x4, matrix products, local_step(): lax.dot_general(g_cur, w_down[layer], COL_CONTRACT, preferred_element_typ...  176 us
    dot_general x4, matrix products, local_step(): jnp.dot(act_val, w_down[layer], preferred_element_type=jnp.float32)  168 us
    dot_general x4, matrix products, local_step(): lax.dot_general(act_val, g_cur, ROW_CONTRACT, preferred_element_type=jnp....  159 us
    dot_general x4, matrix products, local_step(): lax.dot_general(h_in, d_pre, ROW_CONTRACT, preferred_element_type=jnp.flo...  152 us
    unnamed x41, local copies, waits for them, and re-layouts  137 us
    another operation x2, other arithmetic, local_step(): return (jnp.stack(grads_up), jnp.stack(grads_down))  137 us
  transfers between devices with their start and end apart: 5, of which 5 were waited for; matrix products, arithmetic and copies ran while one was open for 8% of the time, Pallas kernels for 0%

commit v1 on v0

v1 whole, which is shorter than its diff:
```python
import functools
import jax
import jax.numpy as jnp
from jax import lax
from jax.sharding import PartitionSpec as P

ROW_CONTRACT = (((0,), (0,)), ((), ()))
COL_CONTRACT = (((1,), (1,)), ((), ()))
CHUNKS = 2


def gelu_tanh(value):
    return jax.nn.gelu(value, approximate=True)


def dot_f32(lhs, rhs):
    return jnp.dot(lhs, rhs, preferred_element_type=jnp.float32)


def scatter_sum(part):
    return lax.psum_scatter(part, "tp", scatter_dimension=0, tiled=True)


def gather_rows(own):
    return lax.all_gather(own, "tp", axis=0, tiled=True)


def local_step(hidden, targets, w_up, w_down, total_tokens):
    layers = w_up.shape[0]
    tp = lax.axis_size("tp")
    me = lax.axis_index("tp")
    rows = hidden.shape[0] // CHUNKS
    own_rows = rows // tp

    def own_slice(arr, chunk):
        return lax.dynamic_slice_in_dim(arr, chunk * rows + me * own_rows, own_rows, 0)

    h_full = [hidden[c * rows:(c + 1) * rows] for c in range(CHUNKS)]
    h_own = [own_slice(hidden, c) for c in range(CHUNKS)]
    t_own = [own_slice(targets, c) for c in range(CHUNKS)]
    saved = []
    g_own = [None] * CHUNKS
    g_full = [None] * CHUNKS
    for layer in range(layers):
        keep = []
        nxt = [None] * CHUNKS
        for c in range(CHUNKS):
            pre = dot_f32(h_full[c], w_up[layer]).astype(jnp.bfloat16)
            act = gelu_tanh(pre.astype(jnp.float32)).astype(jnp.bfloat16)
            part = dot_f32(act, w_down[layer])
            branch = scatter_sum(part).astype(jnp.bfloat16)
            keep.append((h_full[c], pre, act))
            h_own[c] = h_own[c] + branch
            if layer < layers - 1:
                nxt[c] = gather_rows(h_own[c])
            else:
                err = (h_own[c].astype(jnp.float32) - t_own[c].astype(jnp.float32)) / total_tokens
                g_own[c] = err.astype(jnp.bfloat16)
                g_full[c] = gather_rows(g_own[c])
        saved.append(keep)
        h_full = nxt
    grads_up = [None] * layers
    grads_down = [None] * layers
    for layer in reversed(range(layers)):
        nxt = [None] * CHUNKS
        sum_down = 0.0
        sum_up = 0.0
        for c in range(CHUNKS):
            h_in, pre, act = saved[layer][c]
            d_act = lax.dot_general(g_full[c], w_down[layer], COL_CONTRACT, preferred_element_type=jnp.float32)
            _, gelu_vjp = jax.vjp(gelu_tanh, pre.astype(jnp.float32))
            d_pre = gelu_vjp(d_act)[0].astype(jnp.bfloat16)
            if layer > 0:
                back = lax.dot_general(d_pre, w_up[layer], COL_CONTRACT, preferred_element_type=jnp.float32)
                g_own[c] = (g_own[c].astype(jnp.float32) + scatter_sum(back)).astype(jnp.bfloat16)
                nxt[c] = gather_rows(g_own[c])
            saved[layer][c] = (h_in, d_pre, act, g_full[c])
        h_all, d_all, a_all, g_all = [jnp.concatenate([saved[layer][c][i] for c in range(CHUNKS)], 0) for i in range(4)]
        sum_down = lax.dot_general(a_all, g_all, ROW_CONTRACT, preferred_element_type=jnp.float32)
        sum_up = lax.dot_general(h_all, d_all, ROW_CONTRACT, preferred_element_type=jnp.float32)
        grads_down[layer] = lax.psum(sum_down, "dp")
        grads_up[layer] = lax.psum(sum_up, "dp")
        g_full = nxt
    return jnp.stack(grads_up), jnp.stack(grads_down)


def solution(mesh):
    def grad_step(hidden_in, targets, w_up, w_down):
        step_fn = functools.partial(local_step, total_tokens=hidden_in.shape[0])
        mapped = jax.shard_map(step_fn, mesh=mesh, in_specs=(P("dp", None), P("dp", None), P(None, None, "tp"), P(None, "tp", None)), out_specs=(P(None, None, "tp"), P(None, "tp", None)), check_vma=False)
        return mapped(hidden_in, targets, w_up, w_down)

    return grad_step
```

time: 5160 us -> 2920 us (0.57)
  blocking collectives: 2770 us -> 0 us
  waiting for transfers between devices: 1160 us -> 1620 us
  matrix products: 877 us -> 949 us
    psum x4 -> x0, blocking collectives: 2770 us -> none  [local_step(): branch = lax.psum(part_out, 'tp').astype(jnp.bfloat16)]
    reduce_scatter x0 -> x14, waiting for transfers between devices: none -> 994 us  [scatter_sum(): return lax.psum_scatter(part, 'tp', scatter_dimension=0, tiled=True)]
    psum x5 -> x2, waiting for transfers between devices: 1160 us -> 186 us  [the longest x1 106 us: local_step(): grads_up[layer] = lax.psum(sum_up, 'dp')]
    all_gather x0 -> x14, waiting for transfers between devices: none -> 440 us  [gather_rows(): return lax.all_gather(own, 'tp', axis=0, tiled=True)]
    dot_general x20 -> x32, matrix products: 778 us -> 834 us  [the longest x16 358 us: dot_f32(): return jnp.dot(lhs, rhs, preferred_element_type=jnp.float32)]
    dot_general x3 -> x6, matrix products: 99.7 us -> 115 us  [local_step(): lax.dot_general(d_pre, w_up[layer], COL_CONTRACT, preferred_element_type=...]
    unnamed x41 -> x63, local copies, waits for them, and re-layouts: 137 us -> 133 us
  transfers between devices with their start and end apart: 5 -> 30, of which waited for: 5 -> 30; matrix products, arithmetic and copies ran while one was open for 8% -> 36% of each run, Pallas kernels for 0% -> 0%
where the time goes in v1:
time: 2920 us; the launch traced here: 2910 us
  waiting for transfers between devices  1620 us (55%)
  matrix products  949 us (32%)
  other arithmetic  179 us (6%)
  local copies, waits for them, and re-layouts  133 us (5%)
    reduce_scatter x14, waiting for transfers between devices, scatter_sum(): return lax.psum_scatter(part, 'tp', scatter_dimension=0, tiled=True)  994 us
    all_gather x14, waiting for transfers between devices, gather_rows(): return lax.all_gather(own, 'tp', axis=0, tiled=True)  440 us
    dot_general x16, matrix products, dot_f32(): return jnp.dot(lhs, rhs, preferred_element_type=jnp.float32)  358 us
    dot_general x8, matrix products, local_step(): lax.dot_general(g_full[c], w_down[layer], COL_CONTRACT, preferred_element...  196 us
    dot_general x4, matrix products, local_step(): lax.dot_general(h_all, d_all, ROW_CONTRACT, preferred_element_type=jnp.fl...  140 us
    dot_general x4, matrix products, local_step(): lax.dot_general(a_all, g_all, ROW_CONTRACT, preferred_element_type=jnp.fl...  140 us
    another operation x2, other arithmetic, local_step(): return (jnp.stack(grads_up), jnp.stack(grads_down))  137 us
    unnamed x63, local copies, waits for them, and re-layouts  133 us
  transfers between devices with their start and end apart: 30, of which 30 were waited for; matrix products, arithmetic and copies ran while one was open for 36% of the time, Pallas kernels for 0%

profile of v1, /device:TPU:0, one launch (start us, length us, event | category | flops | bytes accessed | tf_op | source)
XLA Modules:
  0.0 2912.1 jit_solution(17929048551136773599)
XLA Ops:
  110.6 44.2 %reduce-scatter.15.cloned.1.call-done = f32[256,2560]{1,0:T(8,128)} async-done(((f32[1024,2560]{1,0:T(8,128)}), f32[256,2560]{1,0:T(8,128)}) %reduce-scatter.15.cloned.1.call-update) | async-done | bytes 2621456 | tf_op jit(solution)/shard_map/reduce_scatter | solution.py:21
  154.9 101.3 %reduce-scatter.29.cloned.1.call-done = f32[256,2560]{1,0:T(8,128)} async-done(((f32[1024,2560]{1,0:T(8,128)}), f32[256,2560]{1,0:T(8,128)}) %reduce-scatter.29.cloned.1.call-update) | async-done | bytes 2621456 | tf_op jit(solution)/shard_map/reduce_scatter | solution.py:21
  262.8 54.7 %all-gather.29.cloned.1.call-done = bf16[1024,2560]{1,0:T(8,128)(2,1)} async-done(((bf16[256,2560]{1,0:T(8,128)(2,1)}), bf16[1024,2560]{1,0:T(8,128)(2,1)}) %all-gather.29.cloned.1.call-update) | async-done | bytes 5242896 | tf_op jit(solution)/shard_map/all_gather | solution.py:25
  422.4 53.5 %reduce-scatter.31.cloned.1.call-done = f32[256,2560]{1,0:T(8,128)} async-done(((f32[1024,2560]{1,0:T(8,128)}), f32[256,2560]{1,0:T(8,128)}) %reduce-scatter.31.cloned.1.call-update) | async-done | bytes 2621456 | tf_op jit(solution)/shard_map/reduce_scatter | solution.py:21
  479.0 98.2 %reduce-scatter.17.cloned.1.call-done = f32[256,2560]{1,0:T(8,128)} async-done(((f32[1024,2560]{1,0:T(8,128)}), f32[256,2560]{1,0:T(8,128)}) %reduce-scatter.17.cloned.1.call-update) | async-done | bytes 2621456 | tf_op jit(solution)/shard_map/reduce_scatter | solution.py:21
  580.2 54.3 %all-gather.31.cloned.1.call-done = bf16[1024,2560]{1,0:T(8,128)(2,1)} async-done(((bf16[256,2560]{1,0:T(8,128)(2,1)}), bf16[1024,2560]{1,0:T(8,128)(2,1)}) %all-gather.31.cloned.1.call-update) | async-done | bytes 5242896 | tf_op jit(solution)/shard_map/all_gather | solution.py:25
  739.6 53.6 %reduce-scatter.33.cloned.1.call-done = f32[256,2560]{1,0:T(8,128)} async-done(((f32[1024,2560]{1,0:T(8,128)}), f32[256,2560]{1,0:T(8,128)}) %reduce-scatter.33.cloned.1.call-update) | async-done | bytes 2621456 | tf_op jit(solution)/shard_map/reduce_scatter | solution.py:21
  796.3 98.1 %reduce-scatter.19.cloned.1.call-done = f32[256,2560]{1,0:T(8,128)} async-done(((f32[1024,2560]{1,0:T(8,128)}), f32[256,2560]{1,0:T(8,128)}) %reduce-scatter.19.cloned.1.call-update) | async-done | bytes 2621456 | tf_op jit(solution)/shard_map/reduce_scatter | solution.py:21
  897.5 54.3 %all-gather.33.cloned.1.call-done = bf16[1024,2560]{1,0:T(8,128)(2,1)} async-done(((bf16[256,2560]{1,0:T(8,128)(2,1)}), bf16[1024,2560]{1,0:T(8,128)(2,1)}) %all-gather.33.cloned.1.call-update) | async-done | bytes 5242896 | tf_op jit(solution)/shard_map/all_gather | solution.py:25
  1056.3 54.1 %reduce-scatter.35.cloned.1.call-done = f32[256,2560]{1,0:T(8,128)} async-done(((f32[1024,2560]{1,0:T(8,128)}), f32[256,2560]{1,0:T(8,128)}) %reduce-scatter.35.cloned.1.call-update) | async-done | bytes 2621456 | tf_op jit(solution)/shard_map/reduce_scatter | solution.py:21
  1110.4 101.2 %reduce-scatter.21.cloned.1.call-done = f32[256,2560]{1,0:T(8,128)} async-done(((f32[1024,2560]{1,0:T(8,128)}), f32[256,2560]{1,0:T(8,128)}) %reduce-scatter.21.cloned.1.call-update) | async-done | bytes 2621456 | tf_op jit(solution)/shard_map/reduce_scatter | solution.py:21
  1218.2 55.1 %all-gather.35.cloned.1.call-done = bf16[1024,2560]{1,0:T(8,128)(2,1)} async-done(((bf16[256,2560]{1,0:T(8,128)(2,1)}), bf16[1024,2560]{1,0:T(8,128)(2,1)}) %all-gather.35.cloned.1.call-update) | async-done | bytes 5242896 | tf_op jit(solution)/shard_map/all_gather | solution.py:25
  1376.0 55.7 %reduce-scatter.37.cloned.1.call-done = f32[256,2560]{1,0:T(8,128)} async-done(((f32[1024,2560]{1,0:T(8,128)}), f32[256,2560]{1,0:T(8,128)}) %reduce-scatter.37.cloned.1.call-update) | async-done | bytes 2621456 | tf_op jit(solution)/shard_map/reduce_scatter | solution.py:21
  1434.9 98.0 %reduce-scatter.23.cloned.1.call-done = f32[256,2560]{1,0:T(8,128)} async-done(((f32[1024,2560]{1,0:T(8,128)}), f32[256,2560]{1,0:T(8,128)}) %reduce-scatter.23.cloned.1.call-update) | async-done | bytes 2621456 | tf_op jit(solution)/shard_map/reduce_scatter | solution.py:21
  1536.2 54.0 %all-gather.37.cloned.1.call-done = bf16[1024,2560]{1,0:T(8,128)(2,1)} async-done(((bf16[256,2560]{1,0:T(8,128)(2,1)}), bf16[1024,2560]{1,0:T(8,128)(2,1)}) %all-gather.37.cloned.1.call-update) | async-done | bytes 5242896 | tf_op jit(solution)/shard_map/all_gather | solution.py:25
  1693.0 55.8 %reduce-scatter.39.cloned.1.call-done = f32[256,2560]{1,0:T(8,128)} async-done(((f32[1024,2560]{1,0:T(8,128)}), f32[256,2560]{1,0:T(8,128)}) %reduce-scatter.39.cloned.1.call-update) | async-done | bytes 2621456 | tf_op jit(solution)/shard_map/reduce_scatter | solution.py:21
  1752.0 98.2 %reduce-scatter.25.cloned.1.call-done = f32[256,2560]{1,0:T(8,128)} async-done(((f32[1024,2560]{1,0:T(8,128)}), f32[256,2560]{1,0:T(8,128)}) %reduce-scatter.25.cloned.1.call-update) | async-done | bytes 2621456 | tf_op jit(solution)/shard_map/reduce_scatter | solution.py:21
  1853.8 53.8 %all-gather.39.cloned.1.call-done = bf16[1024,2560]{1,0:T(8,128)(2,1)} async-done(((bf16[256,2560]{1,0:T(8,128)(2,1)}), bf16[1024,2560]{1,0:T(8,128)(2,1)}) %all-gather.39.cloned.1.call-update) | async-done | bytes 5242896 | tf_op jit(solution)/shard_map/all_gather | solution.py:25
  2010.4 35.4 %convolution_bitcast_fusion.4 = f32[1,2560,2560]{1,2,0:T(8,128)} fusion(bf16[1024,2560]{1,0:T(8,128)(2,1)} %all-gather.33.cloned.1.call-done, bf16[1024,2560]{1,0:T(8,128)(2,1)} %all-gather.19.cloned.1.call-done, bf16[1024,2560]{1,0:T(8,128)(2,1)} %copy-done.21, bf16[1024,2560]{1,0:T(8,128)(2,1)} %copy-done.22), kind=kOutput, calls=%fused_computation.46 | convolution fusion | flops 26885488640 | bytes 47185920 | tf_op jit(solution)/shard_map/dot_general | solution.py:80
  2069.7 35.4 %convolution_bitcast_fusion.5 = f32[1,2560,2560]{1,2,0:T(8,128)} fusion(bf16[1024,2560]{1,0:T(8,128)(2,1)} %all-gather.31.cloned.1.call-done, bf16[1024,2560]{1,0:T(8,128)(2,1)} %all-gather.17.cloned.1.call-done, bf16[1024,2560]{1,0:T(8,128)(2,1)} %copy-done.23, bf16[1024,2560]{1,0:T(8,128)(2,1)} %copy-done.24), kind=kOutput, calls=%fused_computation.47 | convolution fusion | flops 26885488640 | bytes 47185920 | tf_op jit(solution)/shard_map/dot_general | solution.py:80
  2105.1 61.7 %reduce-scatter.27.cloned.1.call-done = f32[256,2560]{1,0:T(8,128)} async-done(((f32[1024,2560]{1,0:T(8,128)}), f32[256,2560]{1,0:T(8,128)}) %reduce-scatter.27.cloned.1.call-update) | async-done | bytes 2621456 | tf_op jit(solution)/shard_map/reduce_scatter | solution.py:21
  2169.9 35.5 %convolution_bitcast_fusion.6 = f32[1,2560,2560]{1,2,0:T(8,128)} fusion(bf16[1024,2560]{1,0:T(8,128)(2,1)} %all-gather.29.cloned.1.call-done, bf16[1024,2560]{1,0:T(8,128)(2,1)} %all-gather.15.cloned.1.call-done, bf16[1024,2560]{1,0:T(8,128)(2,1)} %copy-done.25, bf16[1024,2560]{1,0:T(8,128)(2,1)} %copy-done.26), kind=kOutput, calls=%fused_computation.48 | convolution fusion | flops 26885488640 | bytes 47185920 | tf_op jit(solution)/shard_map/dot_general | solution.py:80
  2307.1 33.9 %convolution_bitcast_fusion.7 = f32[1,2560,2560]{1,2,0:T(8,128)} fusion(bf16[2048,2560]{1,0:T(8,128)(2,1)} %param.4, bf16[1024,2560]{1,0:T(8,128)(2,1)S(1)} %copy-done.12, bf16[1024,2560]{1,0:T(8,128)(2,1)} %fusion.93), kind=kOutput, calls=%fused_computation.49 | convolution fusion | flops 26864517120 | bytes 47185920 | tf_op jit(solution)/shard_map/dot_general | solution.py:80
  2341.1 36.2 %convolution_bitcast_fusion = f32[1,2560,2560]{2,1,0:T(8,128)} fusion(bf16[1024,2560]{1,0:T(8,128)(2,1)} %get-tuple-element.16, bf16[1024,2560]{1,0:T(8,128)(2,1)} %get-tuple-element.18, bf16[1024,2560]{1,0:T(8,128)(2,1)} %all-gather.35.cloned.1.call-done, bf16[1024,2560]{1,0:T(8,128)(2,1)} %all-gather.21.cloned.1.call-done), kind=kOutput, calls=%fused_computation.42 | convolution fusion | flops 26885488640 | bytes 47185920 | tf_op jit(solution)/shard_map/dot_general | solution.py:79
  2377.4 33.9 %convolution_bitcast_fusion.1 = f32[1,2560,2560]{2,1,0:T(8,128)} fusion(bf16[1024,2560]{1,0:T(8,128)(2,1)} %get-tuple-element.20, bf16[1024,2560]{1,0:T(8,128)(2,1)} %get-tuple-element.22, bf16[1024,2560]{1,0:T(8,128)(2,1)S(1)} %bitcast.156, bf16[1024,2560]{1,0:T(8,128)(2,1)} %all-gather.23.cloned.1.call-done), kind=kOutput, calls=%fused_computation.43 | convolution fusion | flops 26885488640 | bytes 47185920 | tf_op jit(solution)/shard_map/dot_general | solution.py:79
  2411.3 35.8 %convolution_bitcast_fusion.2 = f32[1,2560,2560]{2,1,0:T(8,128)} fusion(bf16[1024,2560]{1,0:T(8,128)(2,1)} %get-tuple-element.24, bf16[1024,2560]{1,0:T(8,128)(2,1)} %get-tuple-element.26, bf16[1024,2560]{1,0:T(8,128)(2,1)} %all-gather.39.cloned.1.call-done, bf16[1024,2560]{1,0:T(8,128)(2,1)} %all-gather.25.cloned.1.call-done), kind=kOutput, calls=%fused_computation.44 | convolution fusion | flops 26885488640 | bytes 47185920 | tf_op jit(solution)/shard_map/dot_general | solution.py:79
  2447.1 33.8 %convolution_bitcast_fusion.3 = f32[1,2560,2560]{2,1,0:T(8,128)} fusion(bf16[1024,2560]{1,0:T(8,128)(2,1)} %get-tuple-element.28, bf16[1024,2560]{1,0:T(8,128)(2,1)} %get-tuple-element.30, bf16[1024,2560]{1,0:T(8,128)(2,1)S(1)} %bitcast.158, bf16[1024,2560]{1,0:T(8,128)(2,1)} %all-gather.27.cloned.1.call-done), kind=kOutput, calls=%fused_computation.45 | convolution fusion | flops 26885488640 | bytes 47185920 | tf_op jit(solution)/shard_map/dot_general | solution.py:79
  2480.9 106.0 %all-reduce.5.cloned.1.call-done = (f32[1,2560,2560]{1,2,0:T(8,128)}, f32[1,2560,2560]{1,2,0:T(8,128)}, f32[1,2560,2560]{1,2,0:T(8,128)}, f32[1,2560,2560]{1,2,0:T(8,128)}) async-done(((f32[1,2560,2560]{1,2,0:T(8,128)}, f32[1,2560,2560]{1,2,0:T(8,128)}, f32[1,2560,2560]{1,2,0:T(8,128)}, f32[1,2560,2560]{1,2,0:T(8,128)}), (f32[1,2560,2560]{1,2,0:T(8,128)}, f32[1,2560,2560]{1,2,0:T(8,128)}, ...) | async-done | bytes 104857616 | tf_op jit(solution)/shard_map/psum | solution.py:82
  2586.9 68.5 %pad_maximum_fusion = f32[4,2560,2560]{1,2,0:T(8,128)} fusion(f32[1,2560,2560]{1,2,0:T(8,128)} %get-tuple-element.4, f32[1,2560,2560]{1,2,0:T(8,128)} %get-tuple-element.5, f32[1,2560,2560]{1,2,0:T(8,128)} %get-tuple-element.6, f32[1,2560,2560]{1,2,0:T(8,128)} %get-tuple-element.7), kind=kLoop, calls=%fused_computation | loop fusion | flops 78643200 | bytes 209715200 | tf_op jit(solution)/shard_map/stack | solution.py:84
  2655.4 100.8 %copy.9 = f32[4,2560,2560]{2,1,0:T(8,128)} copy(f32[4,2560,2560]{1,2,0:T(8,128)} %pad_maximum_fusion) | data formatting | bytes 209715200
  2756.2 80.4 %all-reduce.7.cloned.1.call-done = (f32[1,2560,2560]{2,1,0:T(8,128)}, f32[1,2560,2560]{2,1,0:T(8,128)}, f32[1,2560,2560]{2,1,0:T(8,128)}, f32[1,2560,2560]{2,1,0:T(8,128)}) async-done(((f32[1,2560,2560]{2,1,0:T(8,128)}, f32[1,2560,2560]{2,1,0:T(8,128)}, f32[1,2560,2560]{2,1,0:T(8,128)}, f32[1,2560,2560]{2,1,0:T(8,128)}), (f32[1,2560,2560]{2,1,0:T(8,128)}, f32[1,2560,2560]{2,1,0:T(8,128)}, ...) | async-done | bytes 104857616 | tf_op jit(solution)/shard_map/psum | solution.py:81
  2836.6 68.5 %pad_maximum_fusion.1 = f32[4,2560,2560]{2,1,0:T(8,128)} fusion(f32[1,2560,2560]{2,1,0:T(8,128)} %get-tuple-element.8, f32[1,2560,2560]{2,1,0:T(8,128)} %get-tuple-element.9, f32[1,2560,2560]{2,1,0:T(8,128)} %get-tuple-element.10, f32[1,2560,2560]{2,1,0:T(8,128)} %get-tuple-element.11), kind=kLoop, calls=%fused_computation.1 | loop fusion | flops 78643200 | bytes 209715200 | tf_op jit(solution)/shard_map/stack | solution.py:84
  (175 shorter events, 893.2 us)
Async XLA Ops:
  7.2 147.7 %reduce-scatter.15.cloned.1.call-start = ((), (), s32[]{:S(2)}) async-start(), calls=%async_computation.14 | async-start | bytes 13107200 | tf_op jit(solution)/shard_map/reduce_scatter | solution.py:21
  54.2 202.0 %reduce-scatter.29.cloned.1.call-start = ((), (), s32[]{:S(2)}) async-start(), calls=%async_computation.28 | async-start | bytes 13107200 | tf_op jit(solution)/shard_map/reduce_scatter | solution.py:21
  110.5 207.0 %all-gather.29.cloned.1.call-start = ((), (), s32[]{:S(2)}) async-start(), calls=%async_computation.29 | async-start | bytes 6553600 | tf_op jit(solution)/shard_map/all_gather | solution.py:25
  261.8 112.9 %all-gather.15.cloned.1.call-start = ((), (), s32[]{:S(2)}) async-start(), calls=%async_computation.15 | async-start | bytes 6553600 | tf_op jit(solution)/shard_map/all_gather | solution.py:25
  262.4 213.6 %reduce-scatter.31.cloned.1.call-start = ((), (), s32[]{:S(2)}) async-start(), calls=%async_computation.30 | async-start | bytes 13107200 | tf_op jit(solution)/shard_map/reduce_scatter | solution.py:21
  364.5 212.6 %reduce-scatter.17.cloned.1.call-start = ((), (), s32[]{:S(2)}) async-start(), calls=%async_computation.16 | async-start | bytes 13107200 | tf_op jit(solution)/shard_map/reduce_scatter | solution.py:21
  422.0 212.5 %all-gather.31.cloned.1.call-start = ((), (), s32[]{:S(2)}) async-start(), calls=%async_computation.31 | async-start | bytes 6553600 | tf_op jit(solution)/shard_map/all_gather | solution.py:25
  478.9 213.0 %all-gather.17.cloned.1.call-start = ((), (), s32[]{:S(2)}) async-start(), calls=%async_computation.17 | async-start | bytes 6553600 | tf_op jit(solution)/shard_map/all_gather | solution.py:25
  580.1 213.1 %reduce-scatter.33.cloned.1.call-start = ((), (), s32[]{:S(2)}) async-start(), calls=%async_computation.32 | async-start | bytes 13107200 | tf_op jit(solution)/shard_map/reduce_scatter | solution.py:21
  681.8 212.7 %reduce-scatter.19.cloned.1.call-start = ((), (), s32[]{:S(2)}) async-start(), calls=%async_computation.18 | async-start | bytes 13107200 | tf_op jit(solution)/shard_map/reduce_scatter | solution.py:21
  739.2 212.6 %all-gather.33.cloned.1.call-start = ((), (), s32[]{:S(2)}) async-start(), calls=%async_computation.33 | async-start | bytes 6553600 | tf_op jit(solution)/shard_map/all_gather | solution.py:25
  796.3 212.8 %all-gather.19.cloned.1.call-start = ((), (), s32[]{:S(2)}) async-start(), calls=%async_computation.19 | async-start | bytes 6553600 | tf_op jit(solution)/shard_map/all_gather | solution.py:25
  897.4 212.9 %reduce-scatter.35.cloned.1.call-start = ((), (), s32[]{:S(2)}) async-start(), calls=%async_computation.34 | async-start | bytes 13107200 | tf_op jit(solution)/shard_map/reduce_scatter | solution.py:21
  998.8 212.8 %reduce-scatter.21.cloned.1.call-start = ((), (), s32[]{:S(2)}) async-start(), calls=%async_computation.20 | async-start | bytes 13107200 | tf_op jit(solution)/shard_map/reduce_scatter | solution.py:21
  1056.1 217.2 %all-gather.35.cloned.1.call-start = ((), (), s32[]{:S(2)}) async-start(), calls=%async_computation.35 | async-start | bytes 6553600 | tf_op jit(solution)/shard_map/all_gather | solution.py:25
  1217.5 113.0 %all-gather.21.cloned.1.call-start = ((), (), s32[]{:S(2)}) async-start(), calls=%async_computation.21 | async-start | bytes 6553600 | tf_op jit(solution)/shard_map/all_gather | solution.py:25
  1218.1 213.6 %reduce-scatter.37.cloned.1.call-start = ((), (), s32[]{:S(2)}) async-start(), calls=%async_computation.36 | async-start | bytes 13107200 | tf_op jit(solution)/shard_map/reduce_scatter | solution.py:21
  1318.8 214.1 %reduce-scatter.23.cloned.1.call-start = ((), (), s32[]{:S(2)}) async-start(), calls=%async_computation.22 | async-start | bytes 13107200 | tf_op jit(solution)/shard_map/reduce_scatter | solution.py:21
  1375.9 157.0 %copy-start.6 = (bf16[256,2560]{1,0:T(8,128)(2,1)S(1)}, bf16[256,2560]{1,0:T(8,128)(2,1)}, u32[]{:S(2)}) copy-start(bf16[256,2560]{1,0:T(8,128)(2,1)} %get-tuple-element.12) | copy-start | bytes 3932164
  1375.9 214.3 %all-gather.37.cloned.1.call-start = ((), (), s32[]{:S(2)}) async-start(), calls=%async_computation.37 | async-start | bytes 6553600 | tf_op jit(solution)/shard_map/all_gather | solution.py:25
  1434.8 212.7 %all-gather.23.cloned.1.call-start = ((), (), s32[]{:S(2)}) async-start(), calls=%async_computation.23 | async-start | bytes 6553600 | tf_op jit(solution)/shard_map/all_gather | solution.py:25
  1536.0 212.8 %reduce-scatter.39.cloned.1.call-start = ((), (), s32[]{:S(2)}) async-start(), calls=%async_computation.38 | async-start | bytes 13107200 | tf_op jit(solution)/shard_map/reduce_scatter | solution.py:21
  1635.8 214.4 %reduce-scatter.25.cloned.1.call-start = ((), (), s32[]{:S(2)}) async-start(), calls=%async_computation.24 | async-start | bytes 13107200 | tf_op jit(solution)/shard_map/reduce_scatter | solution.py:21
  1693.0 157.2 %copy-start.5 = (bf16[256,2560]{1,0:T(8,128)(2,1)S(1)}, bf16[256,2560]{1,0:T(8,128)(2,1)}, u32[]{:S(2)}) copy-start(bf16[256,2560]{1,0:T(8,128)(2,1)} %add_convert_fusion.5) | copy-start | bytes 3932164
  1693.0 214.6 %all-gather.39.cloned.1.call-start = ((), (), s32[]{:S(2)}) async-start(), calls=%async_computation.39 | async-start | bytes 6553600 | tf_op jit(solution)/shard_map/all_gather | solution.py:25
  1751.9 212.8 %all-gather.25.cloned.1.call-start = ((), (), s32[]{:S(2)}) async-start(), calls=%async_computation.25 | async-start | bytes 6553600 | tf_op jit(solution)/shard_map/all_gather | solution.py:25
  1853.3 212.8 %reduce-scatter.41.cloned.1.call-start = ((), (), s32[]{:S(2)}) async-start(), calls=%async_computation.40 | async-start | bytes 13107200 | tf_op jit(solution)/shard_map/reduce_scatter | solution.py:21
  1953.2 213.6 %reduce-scatter.27.cloned.1.call-start = ((), (), s32[]{:S(2)}) async-start(), calls=%async_computation.26 | async-start | bytes 13107200 | tf_op jit(solution)/shard_map/reduce_scatter | solution.py:21
  2010.4 213.6 %all-gather.41.cloned.1.call-start = ((), (), s32[]{:S(2)}) async-start(), calls=%async_computation.41 | async-start | bytes 6553600 | tf_op jit(solution)/shard_map/all_gather | solution.py:25
  2069.3 212.1 %all-gather.27.cloned.1.call-start = ((), (), s32[]{:S(2)}) async-start(), calls=%async_computation.27 | async-start | bytes 6553600 | tf_op jit(solution)/shard_map/all_gather | solution.py:25
  2169.9 417.0 %all-reduce.5.cloned.1.call-start = ((), (), s32[]{:S(2)}) async-start(), calls=%async_computation.42 | async-start | bytes 209715200 | tf_op jit(solution)/shard_map/psum | solution.py:82
  2341.1 495.5 %all-reduce.7.cloned.1.call-start = ((), (), s32[]{:S(2)}) async-start(), calls=%async_computation.43 | async-start | bytes 209715200 | tf_op jit(solution)/shard_map/psum | solution.py:81
  (29 other events, 1230.9 us)
Sparse Core Ops, SparseCore 0:
  54.3 100.5 reduce-scatter.14
  158.5 97.6 reduce-scatter.28
  261.9 55.5 all-gather.28
  319.1 55.5 all-gather.14
  378.2 97.6 reduce-scatter.30
  479.4 97.6 reduce-scatter.16
  578.9 55.5 all-gather.30
  636.3 55.5 all-gather.16
  695.5 97.6 reduce-scatter.32
  796.7 97.6 reduce-scatter.18
  896.2 55.5 all-gather.32
  953.4 55.5 all-gather.18
  1012.6 97.6 reduce-scatter.34
  1113.9 97.6 reduce-scatter.20
  1217.6 55.5 all-gather.34
  1274.9 55.5 all-gather.20
  1333.9 97.6 reduce-scatter.36
  1435.1 97.6 reduce-scatter.22
  1534.7 55.5 all-gather.36
  1591.9 55.5 all-gather.22
  1651.1 97.6 reduce-scatter.38
  1752.4 97.6 reduce-scatter.24
  1852.0 55.5 all-gather.38
  1909.2 55.5 all-gather.24
  1968.4 97.6 reduce-scatter.40
  2069.0 97.6 reduce-scatter.26
  2168.4 55.5 all-gather.40
  2225.7 55.5 all-gather.26
  2341.2 245.6 all-reduce.4
  2589.6 246.9 all-reduce.6
